TPU v7x, 32 devices: a whole 2x2x4 slice. The times are simulated.
32 devices in a mesh: scen: 8 (over y, x, core), col: 4 (over z).
Axes of the slice: x: 2, y: 2, z: 4, core: 2. Of those that a mesh axis runs over, the one named last changes fastest.
Arguments:
- coef: float32 [4096, 8192], P('scen', 'col'), as said below
- mask: int32 [4096], replicated, may hold values from 0 to 1, as said below
- assign: int32 [512], replicated, may hold values from 0 to 511, each once
Outputs:
- master: float32 [4, 2048, 4096], P('col', 'scen')
Inputs may be any that keep to these rules, and one draw needn't show every extreme that they name: `mask`: in each aligned block of 512 cuts (the cuts of one index of scen) exactly 256 are active. `coef`: magnitudes of rows and of columns differ widely; entries are finite and not zero on every row.
All inputs are finite; a program needn't handle non-finite values.
Results may differ from a plain program's by a relative error of at most 0.00007.
Values sent between devices are 32-bit elements; how exact they have to be, the bound alone decides.
No kernel may reach another device: no remote copies, remote signals or barrier semaphores. Data moves between devices by JAX's collectives and lax.ppermute only.
A program may use at most 128 MiB of HBM per device.

v0:
```python
import jax
import jax.numpy as jnp
from jax import lax
from jax.sharding import PartitionSpec as P

NV = 8192
K = 8
ACT_DEV = 256
EPS = 1e-06


def on_device(coef, mask, assign):
    rows, width = coef.shape
    groups = lax.axis_size("scen")
    slice_width = width // groups
    cut_total = groups * rows
    slot_total = cut_total // K
    active_total = ACT_DEV * groups
    partial_value = jnp.sum(coef * coef, axis=1)
    total = lax.psum(partial_value, "col")
    row_norm = jnp.sqrt(total / NV + EPS)
    device_index = lax.axis_index("scen")
    own_mask = lax.dynamic_slice_in_dim(mask, device_index * rows, rows)
    live = own_mask.astype(jnp.float32)
    scaled = coef / row_norm[:, None] * live[:, None]
    flipped = scaled.T.reshape(groups, slice_width, rows)
    inverse = jnp.argsort(assign, stable=True)
    kept_rows = jnp.argsort(1 - own_mask, stable=True)[:ACT_DEV]
    picked = jnp.take(flipped, kept_rows, axis=2)
    arrived = lax.all_to_all(picked, "scen", split_axis=0, concat_axis=2, tiled=True)
    norm = jnp.sqrt(jnp.sum(arrived * arrived, axis=2, keepdims=True) / active_total + EPS)
    equil = (arrived / norm).reshape(slice_width, groups, ACT_DEV)
    block_masks = mask.reshape(groups, rows)
    chosen = jnp.argsort(1 - block_masks, axis=1, stable=True)[:, :ACT_DEV]
    bundle = min(groups, 8)
    rounds = groups // bundle
    chosen_sets = chosen.reshape(rounds, bundle, ACT_DEV)
    equil_sets = equil.reshape(slice_width, rounds, bundle, ACT_DEV).transpose(1, 0, 2, 3)
    local_rows = jnp.arange(rows, dtype=jnp.int32)

    def place(pair):
        chosen_set, equil_set = pair
        placing = (chosen_set[:, :, None] == local_rows[None, None, :]).astype(jnp.float32)
        return jnp.einsum("sga,gar->sgr", equil_set, placing, precision=lax.Precision.HIGHEST)

    placed = lax.map(place, (chosen_sets, equil_sets))
    whole = placed.transpose(1, 0, 2, 3).reshape(1, slice_width, cut_total)
    slotted = whole.reshape(1, slice_width, slot_total, K)
    return jnp.take(slotted, inverse, axis=2).reshape(1, slice_width, cut_total)


def solution(mesh):
    in_specs = (P("scen", "col"), P(), P())
    out_specs = P("col", "scen", None)
    return jax.shard_map(
        on_device, mesh=mesh, in_specs=in_specs, out_specs=out_specs, check_vma=False
    )
```

profile of v0, /device:TPU:0, one launch (start us, length us, event | category | flops | bytes accessed | tf_op | source)
XLA Modules:
  0.0 95.5 jit_solution(2898095278292690837)
XLA Ops:
  6.5 0.8 dynamic-slice_subtract_fusion
  7.3 3.8 %sort.50 = (s32[512]{0:T(512)}, s32[512]{0:T(512)S(1)}) sort(s32[512]{0:T(512)S(1)} %get-tuple-element.26, s32[512]{0:T(512)S(1)} %iota.20), dimensions={0}, to_apply=%region_2.0 | sort | flops 4608 | bytes 8192 | tf_op jit(solution)/shard_map/jit(argsort)/sort | solution.py:28
  11.1 2.5 %multiply_reduce_fusion = f32[512]{0:T(512)S(1)} fusion(f32[512,2048]{1,0:T(8,128)} %param.3), kind=kLoop, calls=%fused_computation.4 | loop fusion | flops 2096640 | bytes 4196352 | tf_op jit(solution)/shard_map/reduce_sum | solution.py:19
  13.6 13.5 %psum.7 = f32[512]{0:T(512)S(1)} all-reduce(f32[512]{0:T(512)S(1)} %multiply_reduce_fusion), channel_id=1, replica_groups=mesh['scen'=8,'col'=4] {'col'}, use_global_device_ids=true, to_apply=%region_4.5 | all-reduce | flops 512 | bytes 4096 | tf_op jit(solution)/shard_map/psum | solution.py:20
  27.1 2.6 %divide_multiply_fusion = f32[512,2048]{1,0:T(8,128)S(1)} fusion(f32[512,2048]{1,0:T(8,128)} %param.3, f32[512]{0:T(512)S(1)} %get-tuple-element.27, f32[512]{0:T(512)S(1)} %add_sqrt_fusion), kind=kLoop, calls=%fused_computation.3 | loop fusion | flops 2097152 | bytes 8392704 | tf_op jit(solution)/shard_map/mul | solution.py:25
  29.7 4.0 %copy.11 = f32[64,8,8,256]{3,2,1,0:T(8,128)} copy(f32[64,8,8,256]{3,1,2,0:T(8,128)S(1)} %bitcast.25) | data formatting | bytes 8388608
  33.7 2.9 %gather_fusion = f32[256,8,256]{2,1,0:T(8,128)S(1)} fusion(f32[8,256,512]{1,0,2:T(8,128)} %bitcast.26, s32[1024]{0:T(1024)S(1)} %pad_clamp_fusion.1), kind=kCustom, calls=%fused_computation | custom fusion | bytes 4195328 | tf_op jit(solution)/shard_map/jit(_take)/gather | solution.py:29
  36.6 0.3 select_bitcast_fusion
  37.0 2.0 %copy.7 = f32[8,256,256]{1,2,0:T(8,128)} copy(f32[8,256,256]{1,0,2:T(8,128)S(1)} %select_bitcast_fusion) | data formatting | bytes 4194304 | tf_op jit(solution)/shard_map/jit(_take)/select_n | solution.py:29
  39.0 3.7 %all-to-all-start = ((f32[8,256,256]{1,2,0:T(8,128)}), f32[8,256,256]{1,2,0:T(8,128)S(1)}, u32[]{:S(2)}, u32[]{:S(2)}) async-start(f32[8,256,256]{1,2,0:T(8,128)} %copy.7), calls=%async_computation | async-start | bytes 4194304 | tf_op jit(solution)/shard_map/all_to_all | solution.py:30
  42.7 0.0 sort.52.cloned.1.call-start
  42.8 0.6 sub.17
  43.4 0.6 iota.19
  44.0 3.8 %sort.48 = (s32[512]{0:T(512)}, s32[512]{0:T(512)S(1)}) sort(s32[512]{0:T(512)S(1)} %copy-done.1, s32[512]{0:T(512)S(1)} %iota.18), dimensions={0}, to_apply=%region_0.0 | sort | flops 4608 | bytes 8192 | tf_op jit(solution)/shard_map/jit(argsort)/sort | solution.py:27
  47.8 0.1 broadcast_in_dim.39
  47.9 0.2 broadcast_in_dim.40
  48.1 0.5 sort.52.cloned.1.call-done
  48.6 0.7 slice.6
  49.3 20.0 %all-to-all-done = f32[8,256,256]{1,2,0:T(8,128)S(1)} async-done(((f32[8,256,256]{1,2,0:T(8,128)}), f32[8,256,256]{1,2,0:T(8,128)S(1)}, u32[]{:S(2)}, u32[]{:S(2)}) %all-to-all-start) | async-done | bytes 2097184 | tf_op jit(solution)/shard_map/all_to_all | solution.py:30
  69.3 0.3 fusion.1
  69.6 4.5 %fusion = f32[8,512,256]{2,1,0:T(8,128)} fusion(f32[8,256,256]{1,2,0:T(8,128)S(1)} %all-to-all-done, s32[8,256]{1,0:T(8,128)S(1)} %slice.6, f32[256]{0:T(256)S(1)} %add_sqrt_fusion.1), kind=kOutput, calls=%fused_computation.6 | convolution fusion | flops 3222798336 | bytes 6300672 | tf_op jit(solution)/shard_map/while/body/eval_jaxpr/sga,gar->sgr/dot_general | solution.py:44
  74.1 5.1 %gather_fusion.1 = f32[512,256,8]{1,2,0:T(8,128)} fusion(f32[256,512,8]{0,2,1:T(8,128)} %bitcast.24, s32[1024]{0:T(1024)S(1)} %pad_clamp_fusion), kind=kCustom, calls=%fused_computation.1 | custom fusion | bytes 8390656 | tf_op jit(solution)/shard_map/jit(_take)/gather | solution.py:49
  79.2 3.9 %bitcast_select_fusion = f32[1,256,4096]{1,2,0:T(8,128)} fusion(f32[512,256,8]{1,2,0:T(8,128)} %gather_fusion.1, pred[4096]{0:T(1024)(128)(4,1)S(1)} %broadcast_in_dim.40), kind=kLoop, calls=%fused_computation.2 | loop fusion | flops 1048576 | bytes 8392704 | tf_op jit(solution)/shard_map/jit(_take)/select_n | solution.py:49
  83.1 5.6 %copy.9 = f32[1,256,4096]{2,1,0:T(8,128)} copy(f32[1,256,4096]{1,2,0:T(8,128)} %bitcast_select_fusion) | data formatting | bytes 8388608 | tf_op jit(solution)/shard_map/jit(_take)/select_n | solution.py:49
  (16 shorter events, 0.1 us)
Async XLA Ops:
  37.0 5.8 %copy-start = (s32[4096]{0:T(1024)S(1)}, s32[4096]{0:T(1024)}, u32[]{:S(2)}) copy-start(s32[4096]{0:T(1024)} %param.4) | copy-start | bytes 49156
  37.0 7.0 %copy-start.1 = (s32[512]{0:T(512)S(1)}, s32[512]{0:T(512)}, u32[]{:S(2)}) copy-start(s32[512]{0:T(512)} %param.5) | copy-start | bytes 6148
  39.0 30.3 %all-to-all-start = ((f32[8,256,256]{1,2,0:T(8,128)}), f32[8,256,256]{1,2,0:T(8,128)S(1)}, u32[]{:S(2)}, u32[]{:S(2)}) async-start(f32[8,256,256]{1,2,0:T(8,128)} %copy.7), calls=%async_computation | async-start | bytes 4194304 | tf_op jit(solution)/shard_map/all_to_all | solution.py:30
  42.7 5.9 %sort.52.cloned.1.call-start = ((), (), s32[]{:S(2)}) async-start(), calls=%async_computation.1 | async-start | bytes 98336 | tf_op jit(solution)/shard_map/jit(argsort)/sort | solution.py:34
Sparse Core Ops, SparseCore 0:
  45.9 2.4 sort.54.cloned.1.call-done
  (1 shorter events, 0.0 us)
where the time goes:
time: 96.1 us; the launch traced here: 95.5 us
  local copies, waits for them, and re-layouts  22.3 us (23%)
  waiting for transfers between devices  20 us (21%)
  other arithmetic  18 us (19%)
  blocking collectives  13.5 us (14%)
  between operations  13.5 us (14%)
  matrix products  4.46 us (5%)
  starting transfers between devices  3.72 us (4%)
    all_to_all x1, waiting for transfers between devices, on_device(): lax.all_to_all(picked, 'scen', split_axis=0, concat_axis=2, tiled=True)  20 us
    psum x1, blocking collectives, on_device(): total = lax.psum(partial_value, 'col')  13.5 us
    select_n x1, local copies, waits for them, and re-layouts, on_device(): return jnp.take(slotted, inverse, axis=2).reshape(1, slice_width, cut_total)  5.59 us
    gather x1, local copies, waits for them, and re-layouts, on_device(): return jnp.take(slotted, inverse, axis=2).reshape(1, slice_width, cut_total)  5.08 us
    dot_general x1, matrix products, place(): jnp.einsum('sga,gar->sgr', equil_set, placing, precision=lax.Precision.HI...  4.46 us
    unnamed x6, local copies, waits for them, and re-layouts  4 us
    select_n x2, other arithmetic, on_device(): return jnp.take(slotted, inverse, axis=2).reshape(1, slice_width, cut_total)  3.91 us
    sort x1, other arithmetic, on_device(): kept_rows = jnp.argsort(1 - own_mask, stable=True)[:ACT_DEV]  3.77 us
  transfers between devices with their start and end apart: 1, of which 1 were waited for; matrix products, arithmetic and copies ran while one was open for 6% of the time, Pallas kernels for 0%

commit v1 on v0

--- a/solution.py
+++ b/solution.py
@@ -9,6 +9,14 @@
 EPS = 1e-06
 
 
+def added_up(shard, mesh_axis):
+    peers, total = (lax.axis_size(mesh_axis), shard)
+    for far in [1 << k for k in range(peers.bit_length() - 1)]:
+        route = [(i, i ^ far) for i in range(peers)]
+        total = total + lax.ppermute(total, mesh_axis, route)
+    return total
+
+
 def on_device(coef, mask, assign):
     rows, width = coef.shape
     groups = lax.axis_size("scen")
@@ -17,7 +25,7 @@
     slot_total = cut_total // K
     active_total = ACT_DEV * groups
     partial_value = jnp.sum(coef * coef, axis=1)
-    total = lax.psum(partial_value, "col")
+    total = added_up(partial_value, "col")
     row_norm = jnp.sqrt(total / NV + EPS)
     device_index = lax.axis_index("scen")
     own_mask = lax.dynamic_slice_in_dim(mask, device_index * rows, rows)

time: 96.1 us -> 89.5 us (0.931)
  blocking collectives: 13.5 us -> 0 us
  starting transfers between devices: 3.72 us -> 9.49 us
  waiting for transfers between devices: 20 us -> 21.9 us
    psum x1 -> x0, blocking collectives: 13.5 us -> none  [on_device(): total = lax.psum(partial_value, 'col')]
    ppermute x0 -> x2, starting transfers between devices: none -> 5.77 us  [added_up(): total = total + lax.ppermute(total, mesh_axis, route)]
    ppermute x0 -> x2, waiting for transfers between devices: none -> 1.89 us  [added_up(): total = total + lax.ppermute(total, mesh_axis, route)]
  transfers between devices with their start and end apart: 1 -> 3, of which waited for: 1 -> 2; matrix products, arithmetic and copies ran while one was open for 6% -> 11% of each run, Pallas kernels for 0% -> 0%
where the time goes in v1:
time: 89.5 us; the launch traced here: 89 us
  local copies, waits for them, and re-layouts  22.3 us (25%)
  waiting for transfers between devices  21.9 us (24%)
  other arithmetic  17.3 us (19%)
  between operations  13.5 us (15%)
  starting transfers between devices  9.49 us (11%)
  matrix products  4.46 us (5%)
    all_to_all x1, waiting for transfers between devices, on_device(): lax.all_to_all(picked, 'scen', split_axis=0, concat_axis=2, tiled=True)  20 us
    ppermute x2, starting transfers between devices, added_up(): total = total + lax.ppermute(total, mesh_axis, route)  5.77 us
    select_n x1, local copies, waits for them, and re-layouts, on_device(): return jnp.take(slotted, inverse, axis=2).reshape(1, slice_width, cut_total)  5.59 us
    gather x1, local copies, waits for them, and re-layouts, on_device(): return jnp.take(slotted, inverse, axis=2).reshape(1, slice_width, cut_total)  5.08 us
    dot_general x1, matrix products, place(): jnp.einsum('sga,gar->sgr', equil_set, placing, precision=lax.Precision.HI...  4.46 us
    unnamed x6, local copies, waits for them, and re-layouts  3.99 us
    select_n x2, other arithmetic, on_device(): return jnp.take(slotted, inverse, axis=2).reshape(1, slice_width, cut_total)  3.91 us
    sort x1, other arithmetic, on_device(): kept_rows = jnp.argsort(1 - own_mask, stable=True)[:ACT_DEV]  3.77 us
  transfers between devices with their start and end apart: 3, of which 2 were waited for; matrix products, arithmetic and copies ran while one was open for 11% of the time, Pallas kernels for 0%

profile of v1, /device:TPU:0, one launch (start us, length us, event | category | flops | bytes accessed | tf_op | source)
XLA Modules:
  0.0 89.0 jit_solution(12835754770434270107)
XLA Ops:
  6.5 2.5 %multiply_reduce_fusion = f32[512]{0:T(512)S(1)} fusion(f32[512,2048]{1,0:T(8,128)} %param.3), kind=kLoop, calls=%fused_computation.4 | loop fusion | flops 2096640 | bytes 4196352 | tf_op jit(solution)/shard_map/reduce_sum | solution.py:27
  9.1 3.1 %collective-permute-start = (f32[512]{0:T(512)S(1)}, f32[512]{0:T(512)S(1)}, u32[]{:S(2)}, u32[]{:S(2)}) collective-permute-start(f32[512]{0:T(512)S(1)} %multiply_reduce_fusion), channel_id=1, source_target_pairs={{0,1},{1,0},{2,3},{3,2},{4,5},{5,4},{6,7},{7,6},{8,9},{9,8},{10,11... | collective-permute-start | bytes 6152 | tf_op jit(solution)/shard_map/ppermute | solution.py:16
  12.3 3.8 %sort.50 = (s32[512]{0:T(512)}, s32[512]{0:T(512)S(1)}) sort(s32[512]{0:T(512)S(1)} %get-tuple-element.26, s32[512]{0:T(512)S(1)} %iota.20), dimensions={0}, to_apply=%region_2.3 | sort | flops 4608 | bytes 8192 | tf_op jit(solution)/shard_map/jit(argsort)/sort | solution.py:36
  16.1 2.7 %collective-permute-start.1 = (f32[512]{0:T(512)S(1)}, f32[512]{0:T(512)S(1)}, u32[]{:S(2)}, u32[]{:S(2)}) collective-permute-start(f32[512]{0:T(512)S(1)} %add.49), channel_id=1, source_target_pairs={{0,2},{1,3},{2,0},{3,1},{4,6},{5,7},{6,4},{7,5},{8,10},{9,11},{10,... | collective-permute-start | bytes 6152 | tf_op jit(solution)/shard_map/ppermute | solution.py:16
  18.7 1.9 %collective-permute-done.1 = f32[512]{0:T(512)S(1)} collective-permute-done((f32[512]{0:T(512)S(1)}, f32[512]{0:T(512)S(1)}, u32[]{:S(2)}, u32[]{:S(2)}) %collective-permute-start.1) | collective-permute-done | bytes 2080 | tf_op jit(solution)/shard_map/ppermute | solution.py:16
  20.6 2.6 %divide_multiply_fusion = f32[512,2048]{1,0:T(8,128)S(1)} fusion(f32[512,2048]{1,0:T(8,128)} %param.3, f32[512]{0:T(512)S(1)} %get-tuple-element.27, f32[512]{0:T(512)S(1)} %add_sqrt_fusion), kind=kLoop, calls=%fused_computation.3 | loop fusion | flops 2097152 | bytes 8392704 | tf_op jit(solution)/shard_map/mul | solution.py:33
  23.3 4.0 %copy.11 = f32[64,8,8,256]{3,2,1,0:T(8,128)} copy(f32[64,8,8,256]{3,1,2,0:T(8,128)S(1)} %bitcast.25) | data formatting | bytes 8388608
  27.2 2.9 %gather_fusion = f32[256,8,256]{2,1,0:T(8,128)S(1)} fusion(f32[8,256,512]{1,0,2:T(8,128)} %bitcast.26, s32[1024]{0:T(1024)S(1)} %pad_clamp_fusion.1), kind=kCustom, calls=%fused_computation | custom fusion | bytes 4195328 | tf_op jit(solution)/shard_map/jit(_take)/gather | solution.py:37
  30.2 0.3 select_bitcast_fusion
  30.5 2.0 %copy.7 = f32[8,256,256]{1,2,0:T(8,128)} copy(f32[8,256,256]{1,0,2:T(8,128)S(1)} %select_bitcast_fusion) | data formatting | bytes 4194304 | tf_op jit(solution)/shard_map/jit(_take)/select_n | solution.py:37
  32.5 3.7 %all-to-all-start = ((f32[8,256,256]{1,2,0:T(8,128)}), f32[8,256,256]{1,2,0:T(8,128)S(1)}, u32[]{:S(2)}, u32[]{:S(2)}) async-start(f32[8,256,256]{1,2,0:T(8,128)} %copy.7), calls=%async_computation | async-start | bytes 4194304 | tf_op jit(solution)/shard_map/all_to_all | solution.py:38
  36.3 0.6 sub.17
  36.9 0.6 iota.19
  37.5 3.8 %sort.48 = (s32[512]{0:T(512)}, s32[512]{0:T(512)S(1)}) sort(s32[512]{0:T(512)S(1)} %copy-done.1, s32[512]{0:T(512)S(1)} %iota.18), dimensions={0}, to_apply=%region_0.0 | sort | flops 4608 | bytes 8192 | tf_op jit(solution)/shard_map/jit(argsort)/sort | solution.py:35
  41.3 0.1 broadcast_in_dim.39
  41.4 0.2 broadcast_in_dim.40
  41.6 0.5 sort.52.cloned.1.call-done
  42.1 0.7 slice.6
  42.8 20.0 %all-to-all-done = f32[8,256,256]{1,2,0:T(8,128)S(1)} async-done(((f32[8,256,256]{1,2,0:T(8,128)}), f32[8,256,256]{1,2,0:T(8,128)S(1)}, u32[]{:S(2)}, u32[]{:S(2)}) %all-to-all-start) | async-done | bytes 2097184 | tf_op jit(solution)/shard_map/all_to_all | solution.py:38
  62.8 0.3 fusion.1
  63.1 4.5 %fusion = f32[8,512,256]{2,1,0:T(8,128)} fusion(f32[8,256,256]{1,2,0:T(8,128)S(1)} %all-to-all-done, s32[8,256]{1,0:T(8,128)S(1)} %slice.6, f32[256]{0:T(256)S(1)} %add_sqrt_fusion.1), kind=kOutput, calls=%fused_computation.6 | convolution fusion | flops 3222798336 | bytes 6300672 | tf_op jit(solution)/shard_map/while/body/eval_jaxpr/sga,gar->sgr/dot_general | solution.py:52
  67.6 5.1 %gather_fusion.1 = f32[512,256,8]{1,2,0:T(8,128)} fusion(f32[256,512,8]{0,2,1:T(8,128)} %bitcast.24, s32[1024]{0:T(1024)S(1)} %pad_clamp_fusion), kind=kCustom, calls=%fused_computation.1 | custom fusion | bytes 8390656 | tf_op jit(solution)/shard_map/jit(_take)/gather | solution.py:57
  72.7 3.9 %bitcast_select_fusion = f32[1,256,4096]{1,2,0:T(8,128)} fusion(f32[512,256,8]{1,2,0:T(8,128)} %gather_fusion.1, pred[4096]{0:T(1024)(128)(4,1)S(1)} %broadcast_in_dim.40), kind=kLoop, calls=%fused_computation.2 | loop fusion | flops 1048576 | bytes 8392704 | tf_op jit(solution)/shard_map/jit(_take)/select_n | solution.py:57
  76.6 5.6 %copy.9 = f32[1,256,4096]{2,1,0:T(8,128)} copy(f32[1,256,4096]{1,2,0:T(8,128)} %bitcast_select_fusion) | data formatting | bytes 8388608 | tf_op jit(solution)/shard_map/jit(_take)/select_n | solution.py:57
  (20 shorter events, 0.2 us)
Async XLA Ops:
  6.5 5.7 %copy-start = (s32[4096]{0:T(1024)S(1)}, s32[4096]{0:T(1024)}, u32[]{:S(2)}) copy-start(s32[4096]{0:T(1024)} %param.4) | copy-start | bytes 49156
  9.1 7.0 %collective-permute-start = (f32[512]{0:T(512)S(1)}, f32[512]{0:T(512)S(1)}, u32[]{:S(2)}, u32[]{:S(2)}) collective-permute-start(f32[512]{0:T(512)S(1)} %multiply_reduce_fusion), channel_id=1, source_target_pairs={{0,1},{1,0},{2,3},{3,2},{4,5},{5,4},{6,7},{7,6},{8,9},{9,8},{10,11... | collective-permute-start | bytes 6152 | tf_op jit(solution)/shard_map/ppermute | solution.py:16
  16.1 4.5 %collective-permute-start.1 = (f32[512]{0:T(512)S(1)}, f32[512]{0:T(512)S(1)}, u32[]{:S(2)}, u32[]{:S(2)}) collective-permute-start(f32[512]{0:T(512)S(1)} %add.49), channel_id=1, source_target_pairs={{0,2},{1,3},{2,0},{3,1},{4,6},{5,7},{6,4},{7,5},{8,10},{9,11},{10,... | collective-permute-start | bytes 6152 | tf_op jit(solution)/shard_map/ppermute | solution.py:16
  30.5 7.0 %copy-start.1 = (s32[512]{0:T(512)S(1)}, s32[512]{0:T(512)}, u32[]{:S(2)}) copy-start(s32[512]{0:T(512)} %param.5) | copy-start | bytes 6148
  32.5 30.3 %all-to-all-start = ((f32[8,256,256]{1,2,0:T(8,128)}), f32[8,256,256]{1,2,0:T(8,128)S(1)}, u32[]{:S(2)}, u32[]{:S(2)}) async-start(f32[8,256,256]{1,2,0:T(8,128)} %copy.7), calls=%async_computation | async-start | bytes 4194304 | tf_op jit(solution)/shard_map/all_to_all | solution.py:38
  36.2 5.9 %sort.52.cloned.1.call-start = ((), (), s32[]{:S(2)}) async-start(), calls=%async_computation.1 | async-start | bytes 98336 | tf_op jit(solution)/shard_map/jit(argsort)/sort | solution.py:42
Sparse Core Ops, SparseCore 0:
  39.4 2.4 sort.54.cloned.1.call-done
  (1 shorter events, 0.0 us)
